TPU v7x, 32 devices: a whole 2x2x4 slice. The times are simulated.
32 devices in a mesh: plane: 4 (over y, core), line: 8 (over z, x).
Axes of the slice: x: 2, y: 2, z: 4, core: 2. Of those that a mesh axis runs over, the one named last changes fastest.
Arguments:
- flow_state: float32 [5, 64, 1024, 128], P(None, 'plane', 'line'), may hold values from -6 to 6
- wave_speed: float32 [64, 1024, 128], P('plane', 'line'), may hold values from 0.3 to 3
- left_eig: float32 [5, 5], replicated, may hold values from -2.5 to 2.5
- right_eig: float32 [5, 5], replicated, may hold values from -2.5 to 2.5
- lower_inverse: float32 [5, 64, 1024, 128], P(None, 'plane', 'line')
- upper_inverse: float32 [5, 64, 1024, 128], P(None, 'plane', 'line')
- lower_link: float32 [3, 5, 64, 8, 128], P(None, None, 'plane', 'line'), may hold values from 0.29 to 0.33
- upper_link: float32 [3, 5, 64, 8, 128], P(None, None, 'plane', 'line'), may hold values from 0.29 to 0.33
- donor_rows: int32 [4, 8, 4, 32], P('plane', 'line'), may hold values from 0 to 1919
- stencil_offsets: int32 [4, 8, 4, 32], P('plane', 'line'), may hold values from 1 to 128, as said below
- donor_weights: float32 [2, 4, 8, 4, 32], P(None, 'plane', 'line'), may hold values from 0.2 to 0.8
- block_counts: int32 [4, 8, 4], P(None, 'line', 'plane'), may hold values from 8 to 32, as said below
- receptor_rows: int32 [4, 8, 4, 32], P('plane', 'line'), may hold values from 0 to 2047, as said below
Outputs:
- next_state: float32 [5, 64, 1024, 128], P(None, 'plane', 'line')
Inputs may be any that keep to these rules, and one draw needn't show every extreme that they name: `donor_rows`: a donor row leaves room for the stencil offset inside its block. `stencil_offsets`: each offset is 1 or 128. `block_counts`: at most 32 blocks from one source block to one owner; in every line block one owner receives 32 from every source. `receptor_rows`: on each receptor block the rows of all sources and slots are distinct.
All inputs are finite; a program needn't handle non-finite values.
Results may differ from a plain program's by a relative error of at most 0.00014.
Values sent between devices are 32-bit elements; how exact they have to be, the bound alone decides.
A program may use at most 128 MiB of HBM per device.

v0:
```python
import functools
import jax
import jax.numpy as jnp
from jax import lax
from jax.experimental import pallas as pl
from jax.experimental.pallas import tpu as pltpu
from jax.sharding import PartitionSpec as P

MESH = pl.DeviceIdType.MESH
F32 = jnp.float32
BF16 = jnp.bfloat16
PAD = 8
SUB = 8


def split(x):
    hi = x.astype(BF16)
    lo = (x - hi.astype(F32)).astype(BF16)
    return hi, lo


def wide(x):
    hi, lo = split(x)
    both = jnp.concatenate([hi, lo], axis=1)
    return jnp.concatenate([both, both], axis=0)


def product(left_pair, x):
    n = x.shape[1]
    full = jnp.dot(left_pair, wide(x), preferred_element_type=F32)
    return full[:, :n] + full[:, n:]


def kernel(
    np_, nl_, flow, wave, lower, upper, left_eig, right_eig, llink, ulink, drows, doffs, dwts, counts, rrows,
    out,
    ext, wbuf, lbuf, ubuf, lsp, usp, char, obuf, lhs, dsend, drecv, rhs, hsend, hrecv, wedge, cfix,
    amine, atheirs, bmine, btheirs, fin, fsend, ubrow, cor, acor, rows,
    lsem, osem, dsend_s, drecv_s, dloc_s, hsend_s, hrecv_s, asend_s, arecv_s, bsend_s, brecv_s, csend_s, crecv_s,
):
    nv, planes, points, width = lower.shape
    chunks = planes // SUB
    cap = drows.shape[3]
    me = lax.axis_index("plane")
    l = lax.axis_index("line")
    z = l // 2
    x = l % 2
    nz = nl_ // 2
    partner = l + 1 - 2 * x

    barrier = pltpu.get_barrier_semaphore()
    own_chip = me // 2
    peers = [((own_chip + 1 + i) % (np_ // 2)) * 2 + c for i in range(np_ // 2 - 1) for c in (0, 1)]
    peers.append(own_chip * 2 + 1 - me % 2)
    for d in peers:
        pl.semaphore_signal(barrier, inc=1, device_id=(d, l), device_id_type=MESH)
    for step in (1, 2):
        @pl.when(l >= step)
        def _():
            pl.semaphore_signal(barrier, inc=1, device_id=(me, l - step), device_id_type=MESH)

        @pl.when(l + step < nl_)
        def _():
            pl.semaphore_signal(barrier, inc=1, device_id=(me, l + step), device_id_type=MESH)

    flow_in = pltpu.make_async_copy(flow, ext.at[:, :, pl.ds(PAD, points), :], lsem.at[0])
    lower_in = pltpu.make_async_copy(lower, lbuf, lsem.at[1])
    upper_in = pltpu.make_async_copy(upper, ubuf, lsem.at[2])
    wave_in = pltpu.make_async_copy(wave, wbuf, lsem.at[3])
    flow_in.start()
    lower_in.start()
    upper_in.start()
    wave_in.start()

    near = jnp.minimum(l, 2) + jnp.minimum(nl_ - 1 - l, 2)
    pl.semaphore_wait(barrier, len(peers) + near)

    flow_in.wait()

    def gather(d):
        def one(c, carry):
            k1 = drows[0, 0, d, c]
            k2 = k1 + doffs[0, 0, d, c]
            w1 = dwts[0, 0, 0, d, c]
            w2 = dwts[1, 0, 0, d, c]
            p1 = lax.div(k1, points)
            n1 = lax.rem(k1, points) + PAD
            p2 = lax.div(k2, points)
            n2 = lax.rem(k2, points) + PAD
            for v in range(nv):
                dsend[d, v, pl.ds(c, 1), :] = w1 * ext[v, p1, pl.ds(n1, 1), :] + w2 * ext[v, p2, pl.ds(n2, 1), :]
            return carry

        lax.fori_loop(0, cap, one, 0, unroll=4)

    def donor_copy(d):
        return pltpu.make_async_remote_copy(
            src_ref=dsend.at[d], dst_ref=drecv.at[me], send_sem=dsend_s.at[d], recv_sem=drecv_s.at[me],
            device_id=(d, l), device_id_type=MESH)

    for d in peers:
        gather(d)
        donor_copy(d).start()
    gather(me)
    local_copy = pltpu.make_async_copy(dsend.at[me], drecv.at[me], dloc_s.at[0])
    local_copy.start()

    lane = lax.broadcasted_iota(jnp.int32, (points, width), 1)
    row = lax.broadcasted_iota(jnp.int32, (points, width), 0)
    lane1 = lax.broadcasted_iota(jnp.int32, (1, width), 1)
    mix = []
    for v in range(nv):
        m = jnp.zeros((1, width), F32)
        for u in range(nv):
            m = jnp.where(lane1 // 4 == u, -right_eig[v, u], m)
        mix.append(m)

    zero_pad = jnp.zeros((PAD, width), F32)
    lower_in.wait()
    upper_in.wait()

    def spread(block, r, c):
        return jnp.broadcast_to(block[r:r + 1, c:c + 1], (1, width))

    last = points - 1

    def prepare(p, carry):
        at = pl.ds(p, 1)
        packed = jnp.zeros((points, width), F32)
        for v in range(nv):
            ext[v, p, 0:PAD, :] = zero_pad
            ext[v, p, PAD + points:PAD + points + PAD, :] = zero_pad
            lo_block = lbuf[v, p]
            up_block = ubuf[v, p]
            h, o = split(lo_block)
            lsp[v, p, :, 0:points] = h
            lsp[v, p, :, points:2 * points] = o
            h, o = split(up_block)
            usp[v, p, :, 0:points] = h
            usp[v, p, :, points:2 * points] = o
            acor[0, 0, v, at, :] = spread(lo_block, last, 0)
            acor[0, 1, v, at, :] = spread(lo_block, last, 1)
            acor[0, 2, v, at, :] = spread(lo_block, last - 1, 0)
            acor[0, 3, v, at, :] = spread(lo_block, last - 1, 1)
            acor[1, 0, v, at, :] = spread(up_block, 0, last)
            acor[1, 1, v, at, :] = spread(up_block, 0, last - 1)
            acor[1, 2, v, at, :] = spread(up_block, 1, last)
            acor[1, 3, v, at, :] = spread(up_block, 1, last - 1)
            rolled = pltpu.roll(lo_block, 4 * v, 1) if v else lo_block
            unit = ((lane == 4 * v + 2) & (row == last)) | ((lane == 4 * v + 3) & (row == last - 1))
            cols = jnp.where((lane == 4 * v) | (lane == 4 * v + 1), rolled, jnp.where(unit, 1.0, 0.0))
            packed = packed + product(jnp.concatenate([h, o], axis=1), cols)
        for v in range(nv):
            for j in range(2):
                for k in range(2):
                    cor[j, k, v, at, :] = spread(packed, j, 4 * v + k)
            scaled = packed * mix[v]
            h, o = split(scaled)
            hf = h.astype(F32)
            stacked = hf + pltpu.roll(o.astype(F32), 32, 1) + pltpu.roll(hf, 64, 1)
            lhs[p, v * points:(v + 1) * points, :] = stacked.astype(BF16)
        return carry

    lax.fori_loop(0, planes, prepare, 0)

    for side, link in ((0, llink), (1, ulink)):
        for v in range(nv):
            c0, c1, c2 = link[0, v], link[1, v], link[2, v]
            a00, a01, a10, a11 = (acor[side, i, v] for i in range(4))
            amine[side, 0, v] = -(a00 * c0 + a01 * c2)
            amine[side, 1, v] = -a00 * c1
            amine[side, 2, v] = -(a10 * c0 + a11 * c2)
            amine[side, 3, v] = -a10 * c1

    def swap_copy(src, dst, send, recv):
        return pltpu.make_async_remote_copy(src_ref=src, dst_ref=dst, send_sem=send, recv_sem=recv,
                                            device_id=(me, partner), device_id_type=MESH)

    map_copies = [swap_copy(amine.at[s], atheirs.at[s], asend_s.at[s], arecv_s.at[s]) for s in range(2)]
    for copy in map_copies:
        copy.start()

    for d in peers:
        pltpu.make_async_remote_copy(
            src_ref=dsend.at[d], dst_ref=drecv.at[d], send_sem=dsend_s.at[d], recv_sem=drecv_s.at[d],
            device_id=(d, l), device_id_type=MESH).wait_recv()
    local_copy.wait()
    slots = np_ * cap
    for s in range(np_):
        for v in range(nv):
            h, o = split(drecv[s, v])
            rhs[s * cap:(s + 1) * cap, v * width:(v + 1) * width] = h
            rhs[slots + s * cap:slots + (s + 1) * cap, v * width:(v + 1) * width] = o
    rhs[0:slots, nv * width:(nv + 1) * width] = jnp.ones((slots, width), BF16)
    rhs[slots:2 * slots, nv * width:(nv + 1) * width] = jnp.zeros((slots, width), BF16)
    slot_lane = lax.broadcasted_iota(jnp.int32, (1, cap), 1)
    targets = jnp.concatenate(
        [jnp.where(slot_lane < counts[s, 0, 0], rrows[0, 0, s:s + 1, :], planes * points) for s in range(np_)], axis=1)
    target_all = jnp.broadcast_to(targets, (points, slots))
    row_slot = lax.broadcasted_iota(jnp.int32, (points, slots), 0)
    wave_in.wait()

    def scatter(p, carry):
        hot = jnp.where(target_all == row_slot + p * points, 1.0, 0.0).astype(BF16)
        hot2 = jnp.concatenate([hot, hot], axis=1)
        vals = jnp.dot(hot2, rhs[...], preferred_element_type=F32)
        taken = vals[:, nv * width:] > 0.5
        at = pl.ds(p, 1)
        for v in range(nv):
            new = jnp.where(taken, vals[:, v * width:(v + 1) * width], ext[v, p, PAD:PAD + points, :])
            ext[v, p, PAD:PAD + points, :] = new
            for j in range(2):
                hsend[0, j, v, at, :] = new[j:j + 1]
                hsend[1, j, v, at, :] = new[last - j:last - j + 1]
        wedge[0, at, :] = wbuf[p, 0:1, :]
        wedge[1, at, :] = wbuf[p, 1:2, :]
        wedge[2, at, :] = wbuf[p, last:last + 1, :]
        wedge[3, at, :] = wbuf[p, last - 1:last, :]
        return carry

    lax.fori_loop(0, planes, scatter, 0)

    down_copy = pltpu.make_async_remote_copy(src_ref=hsend.at[0], dst_ref=hrecv.at[1], send_sem=hsend_s.at[0],
                                             recv_sem=hrecv_s.at[1], device_id=(me, l - 1), device_id_type=MESH)
    up_copy = pltpu.make_async_remote_copy(src_ref=hsend.at[1], dst_ref=hrecv.at[0], send_sem=hsend_s.at[1],
                                           recv_sem=hrecv_s.at[0], device_id=(me, l + 1), device_id_type=MESH)

    @pl.when(l > 0)
    def _():
        down_copy.start()

    @pl.when(l < nl_ - 1)
    def _():
        up_copy.start()

    @pl.when(l == 0)
    def _():
        hrecv[0] = jnp.zeros(hrecv.shape[1:], F32)

    @pl.when(l == nl_ - 1)
    def _():
        hrecv[1] = jnp.zeros(hrecv.shape[1:], F32)

    piece = 32
    lane_p = lax.broadcasted_iota(jnp.int32, (piece, width), 1)
    first_lane = lane_p == 0
    final_lane = lane_p == width - 1

    def derive(p, carry):
        for part in range(points // piece):
            base = part * piece
            ws = -wbuf[p, base:base + piece, :]
            tends = []
            for u in range(nv):
                o = PAD + base
                mid = ext[u, p, o:o + piece, :]
                n1 = ext[u, p, o + 1:o + 1 + piece, :]
                n2 = ext[u, p, o + 2:o + 2 + piece, :]
                b1 = ext[u, p, o - 1:o - 1 + piece, :]
                b2 = ext[u, p, o - 2:o - 2 + piece, :]
                right = jnp.where(final_lane, 0.0, pltpu.roll(mid, width - 1, 1))
                left = jnp.where(first_lane, 0.0, pltpu.roll(mid, 1, 1))
                total = 0.5 * (right - left) + 0.25 * n1 - 0.75 * b1 + 0.375 * mid + 0.0625 * (n2 + b2)
                tends.append(ws * total)
            for v in range(nv):
                acc = left_eig[v, 0] * tends[0]
                for u in range(1, nv):
                    acc = acc + left_eig[v, u] * tends[u]
                char[v, p, base:base + piece, :] = acc
        return carry

    lax.fori_loop(0, planes, derive, 0)

    @pl.when(l > 0)
    def _():
        up_copy.wait_recv()

    @pl.when(l < nl_ - 1)
    def _():
        down_copy.wait_recv()

    tb1 = [hrecv[0, 0, u] for u in range(nv)]
    tb2 = [hrecv[0, 1, u] for u in range(nv)]
    ta1 = [hrecv[1, 0, u] for u in range(nv)]
    ta2 = [hrecv[1, 1, u] for u in range(nv)]
    for v in range(nv):
        acc = [jnp.zeros((planes, width), F32) for _ in range(4)]
        for u in range(nv):
            e = left_eig[v, u]
            acc[0] = acc[0] + e * (-0.75 * tb1[u] + 0.0625 * tb2[u])
            acc[1] = acc[1] + e * (0.0625 * tb1[u])
            acc[2] = acc[2] + e * (0.25 * ta1[u] + 0.0625 * ta2[u])
            acc[3] = acc[3] + e * (0.0625 * ta1[u])
        for j in range(4):
            cfix[j, v] = -wedge[j] * acc[j]

    def lower_pass(p, carry):
        chunk = p // SUB
        at = pl.ds(p % SUB, 1)
        here = pl.ds(p, 1)
        for v in range(nv):
            for j, r in enumerate((0, 1, last, last - 1)):
                char[v, p, r:r + 1, :] = char[v, p, r:r + 1, :] + cfix[j, v, here, :]
            y = product(lsp[v, p], char[v, p])
            char[v, p] = y
            bmine[0, chunk, 0, v, at, :] = y[last:last + 1]
            bmine[0, chunk, 1, v, at, :] = y[last - 1:last]
        return carry

    def b_copy(side, c):
        return swap_copy(bmine.at[side, c], btheirs.at[side, c], bsend_s.at[side, c], brecv_s.at[side, c])

    for c in range(chunks):
        lax.fori_loop(c * SUB, (c + 1) * SUB, lower_pass, 0)
        b_copy(0, c).start()

    for copy in map_copies:
        copy.wait_recv()

    def chain_copy(side, c):
        to = l + 2 if side == 0 else l - 2
        return pltpu.make_async_remote_copy(
            src_ref=fsend.at[side, c], dst_ref=fin.at[side, c], send_sem=csend_s.at[side, c],
            recv_sem=crecv_s.at[side, c], device_id=(me, to), device_id_type=MESH)

    def has_before(side):
        return z > 0 if side == 0 else z < nz - 1

    def has_after(side):
        return z < nz - 1 if side == 0 else z > 0

    def relay(side, c):
        b_copy(side, c).wait_recv()
        second = x == 1 if side == 0 else x == 0

        @pl.when(has_before(side))
        def _():
            chain_copy(side, c).wait_recv()

        @pl.when(jnp.logical_not(has_before(side)))
        def _():
            fin[side, c] = jnp.zeros(fin.shape[2:], F32)

        sl = slice(c * SUB, (c + 1) * SUB)
        for v in range(nv):
            y1, y2 = fin[side, c, 0, v], fin[side, c, 1, v]
            am = [amine[side, i, v, sl] for i in range(4)]
            at_ = [atheirs[side, i, v, sl] for i in range(4)]
            bm = [bmine[side, c, i, v] for i in range(2)]
            bt = [btheirs[side, c, i, v] for i in range(2)]
            a1 = [jnp.where(second, t, m) for m, t in zip(am, at_)]
            a2 = [jnp.where(second, m, t) for m, t in zip(am, at_)]
            b1 = [jnp.where(second, t, m) for m, t in zip(bm, bt)]
            b2 = [jnp.where(second, m, t) for m, t in zip(bm, bt)]
            m1 = a1[0] * y1 + a1[1] * y2 + b1[0]
            m2 = a1[2] * y1 + a1[3] * y2 + b1[1]
            fsend[side, c, 0, v] = a2[0] * m1 + a2[1] * m2 + b2[0]
            fsend[side, c, 1, v] = a2[2] * m1 + a2[3] * m2 + b2[1]
            fin[side, c, 0, v] = jnp.where(second, m1, y1)
            fin[side, c, 1, v] = jnp.where(second, m2, y2)

        @pl.when(has_after(side))
        def _():
            chain_copy(side, c).start()

    def upper_pass(p, carry):
        here = pl.ds(p, 1)
        for v in range(nv):
            y = product(usp[v, p], char[v, p])
            char[v, p] = y
            ubrow[0, v, here, :] = y[0:1]
            ubrow[1, v, here, :] = y[1:2]
        for part in range(points // piece):
            base = part * piece
            ups = [char[u, p, base:base + piece, :] for u in range(nv)]
            for v in range(nv):
                acc = ext[v, p, PAD + base:PAD + base + piece, :]
                for u in range(nv):
                    acc = acc + right_eig[v, u] * ups[u]
                obuf[v, p, base:base + piece, :] = acc
        return carry

    def back_offset(c):
        sl = slice(c * SUB, (c + 1) * SUB)
        for v in range(nv):
            y1, y2 = fin[0, c, 0, v], fin[0, c, 1, v]
            f = llink[0, v, sl] * y1 + llink[1, v, sl] * y2
            s = llink[2, v, sl] * y1
            rows[c, 4 * v] = f
            rows[c, 4 * v + 1] = s
            for j in range(2):
                bmine[1, c, j, v] = ubrow[j, v, sl] - cor[j, 0, v, sl] * f - cor[j, 1, v, sl] * s
        b_copy(1, c).start()

    for c in range(chunks):
        lax.fori_loop(c * SUB, (c + 1) * SUB, upper_pass, 0)
        relay(0, c)
        back_offset(c)

    nk = 4 * nv
    out_copies = []
    for c in range(chunks):
        relay(1, c)
        sl = slice(c * SUB, (c + 1) * SUB)
        for v in range(nv):
            x1, x2 = fin[1, c, 0, v], fin[1, c, 1, v]
            rows[c, 4 * v + 2] = ulink[0, v, sl] * x1 + ulink[1, v, sl] * x2
            rows[c, 4 * v + 3] = ulink[2, v, sl] * x1

        def finish(q, carry):
            p = c * SUB + q
            r = jnp.concatenate([rows[c, k, pl.ds(q, 1), :] for k in range(nk)]
                                + [jnp.zeros((32 - nk, width), F32)], axis=0)
            h = r.astype(BF16).astype(F32)
            o = r - h
            right = jnp.concatenate([h, h, o, jnp.zeros((width - 96, width), F32)], axis=0).astype(BF16)
            for v in range(nv):
                add = jnp.dot(lhs[p, v * points:(v + 1) * points, :], right, preferred_element_type=F32)
                obuf[v, p] = obuf[v, p] + add
            return carry

        lax.fori_loop(0, SUB, finish, 0)
        copy = pltpu.make_async_copy(obuf.at[:, pl.ds(c * SUB, SUB)], out.at[:, pl.ds(c * SUB, SUB)], osem.at[c])
        copy.start()
        out_copies.append(copy)

    for d in peers:
        donor_copy(d).wait_send()
    for copy in map_copies:
        copy.wait_send()

    @pl.when(l > 0)
    def _():
        down_copy.wait_send()

    @pl.when(l < nl_ - 1)
    def _():
        up_copy.wait_send()

    for side in range(2):
        for c in range(chunks):
            b_copy(side, c).wait_send()

            @pl.when(has_after(side))
            def _():
                chain_copy(side, c).wait_send()
    for copy in out_copies:
        copy.wait()


def local(np_, nl_, flow_state, wave_speed, left_eig, right_eig, lower_inverse, upper_inverse, lower_link, upper_link,
          donor_rows, stencil_offsets, donor_weights, block_counts, receptor_rows):
    nv, planes, points, width = flow_state.shape
    chunks = planes // SUB
    cap = donor_rows.shape[3]
    slots = np_ * cap
    vmem = pl.BlockSpec(memory_space=pltpu.VMEM)
    smem = pl.BlockSpec(memory_space=pltpu.SMEM)
    hbm = pl.BlockSpec(memory_space=pl.ANY)
    dma = pltpu.SemaphoreType.DMA
    state = (2, chunks, 2, nv, SUB, width)
    return pl.pallas_call(
        functools.partial(kernel, np_, nl_),
        out_shape=jax.ShapeDtypeStruct(flow_state.shape, F32),
        in_specs=[hbm, hbm, hbm, hbm, smem, smem, vmem, vmem, smem, smem, smem, smem, vmem],
        out_specs=hbm,
        scratch_shapes=[
            pltpu.VMEM((nv, planes, points + 2 * PAD, width), F32),
            pltpu.VMEM((planes, points, width), F32),
            pltpu.VMEM((nv, planes, points, points), F32),
            pltpu.VMEM((nv, planes, points, points), F32),
            pltpu.VMEM((nv, planes, points, 2 * points), BF16),
            pltpu.VMEM((nv, planes, points, 2 * points), BF16),
            pltpu.VMEM((nv, planes, points, width), F32),
            pltpu.VMEM((nv, planes, points, width), F32),
            pltpu.VMEM((planes, nv * points, width), BF16),
            pltpu.VMEM((np_, nv, cap, width), F32),
            pltpu.VMEM((np_, nv, cap, width), F32),
            pltpu.VMEM((2 * slots, (nv + 1) * width), BF16),
            pltpu.VMEM((2, 2, nv, planes, width), F32),
            pltpu.VMEM((2, 2, nv, planes, width), F32),
            pltpu.VMEM((4, planes, width), F32),
            pltpu.VMEM((4, nv, planes, width), F32),
            pltpu.VMEM((2, 4, nv, planes, width), F32),
            pltpu.VMEM((2, 4, nv, planes, width), F32),
            pltpu.VMEM(state, F32),
            pltpu.VMEM(state, F32),
            pltpu.VMEM(state, F32),
            pltpu.VMEM(state, F32),
            pltpu.VMEM((2, nv, planes, width), F32),
            pltpu.VMEM((2, 2, nv, planes, width), F32),
            pltpu.VMEM((2, 4, nv, planes, width), F32),
            pltpu.VMEM((chunks, 4 * nv, SUB, width), F32),
            dma((4,)), dma((chunks,)), dma((np_,)), dma((np_,)), dma((1,)), dma((2,)), dma((2,)), dma((2,)), dma((2,)),
            dma((2, chunks)), dma((2, chunks)), dma((2, chunks)), dma((2, chunks)),
        ],
        compiler_params=pltpu.CompilerParams(
            collective_id=0, has_side_effects=True, vmem_limit_bytes=60 * 1024 * 1024),
    )(flow_state, wave_speed, lower_inverse, upper_inverse, left_eig, right_eig,
      lower_link.reshape(lower_link.shape[:3] + (width,)), upper_link.reshape(upper_link.shape[:3] + (width,)),
      donor_rows, stencil_offsets, donor_weights, block_counts, receptor_rows)


def solution(mesh):
    in_specs = (
        P(None, "plane", "line", None),
        P("plane", "line", None),
        P(),
        P(),
        P(None, "plane", "line", None),
        P(None, "plane", "line", None),
        P(None, None, "plane", "line", None),
        P(None, None, "plane", "line", None),
        P("plane", "line", None, None),
        P("plane", "line", None, None),
        P(None, "plane", "line", None, None),
        P(None, "line", "plane"),
        P("plane", "line", None, None),
    )
    out_specs = P(None, "plane", "line", None)
    body = functools.partial(local, mesh.shape["plane"], mesh.shape["line"])
    return jax.shard_map(body, mesh=mesh, in_specs=in_specs, out_specs=out_specs, check_vma=False)
```

profile of v0, /device:TPU:0, one launch (start us, length us, event | category | flops | bytes accessed | tf_op | source)
XLA Modules:
  0.0 68.3 jit_solution(11249526817087046360)
XLA Ops:
  0.0 1.3 %copy.14.counts = s32[4,1,1]{2,1,0:T(1,128)} copy(s32[4,1,1]{0,2,1:T(1,128)} %param.24) | data formatting | bytes 32 | tf_op args[11]
  1.3 61.5 %shard_map.127 = f32[5,16,128,128]{3,2,1,0:T(8,128)} custom-call(f32[5,16,128,128]{3,2,1,0:T(8,128)} %flow.1, f32[16,128,128]{2,1,0:T(8,128)} %wave.1, f32[5,16,128,128]{3,2,1,0:T(8,128)} %lower.1, f32[5,16,128,128]{3,2,1,0:T(8,128)} %upper.1, f32[5,5]{1,0:T(8,128)} %left_eig.1, f32[5,5]{1,0:T(8,128)} %right_eig.1, f32[3,5,16,128]{3,2,1,0:T(8,128)} %bitcast.2, ...), custom_call_target="tpu_custom_call" | custom-call | tf_op jit(solution)/shard_map/pallas_call | solution.py:462
  62.8 5.5 %copy.16 = f32[5,16,128,128]{3,2,1,0:T(8,128)} copy(f32[5,16,128,128]{3,2,1,0:T(8,128)} %shard_map.127) | data formatting | bytes 10485760
where the time goes:
time: 68.4 us; the launch traced here: 68.3 us
  Pallas kernels  61.5 us (90%)
  local copies, waits for them, and re-layouts  6.8 us (10%)
    pallas_call x1, Pallas kernels, local(): pl.pallas_call(functools.partial(kernel, np_, nl_), out_shape=jax.ShapeDt...  61.5 us
    unnamed x2, local copies, waits for them, and re-layouts  6.8 us

commit v1 on v0

--- a/solution.py
+++ b/solution.py
@@ -33,10 +33,10 @@
 
 def kernel(
     np_, nl_, flow, wave, lower, upper, left_eig, right_eig, llink, ulink, drows, doffs, dwts, counts, rrows,
-    out,
-    ext, wbuf, lbuf, ubuf, lsp, usp, char, obuf, lhs, dsend, drecv, rhs, hsend, hrecv, wedge, cfix,
+    obuf,
+    ext, wbuf, lbuf, ubuf, lsp, usp, char, packs, lhs, dsend, drecv, rhs, hsend, hrecv, wedge, cfix,
     amine, atheirs, bmine, btheirs, fin, fsend, ubrow, cor, acor, rows,
-    lsem, osem, dsend_s, drecv_s, dloc_s, hsend_s, hrecv_s, asend_s, arecv_s, bsend_s, brecv_s, csend_s, crecv_s,
+    lsem, dsend_s, drecv_s, dloc_s, hsend_s, hrecv_s, asend_s, arecv_s, bsend_s, brecv_s, csend_s, crecv_s,
 ):
     nv, planes, points, width = lower.shape
     chunks = planes // SUB
@@ -126,7 +126,6 @@
 
     def prepare(p, carry):
         at = pl.ds(p, 1)
-        packed = jnp.zeros((points, width), F32)
         for v in range(nv):
             ext[v, p, 0:PAD, :] = zero_pad
             ext[v, p, PAD + points:PAD + points + PAD, :] = zero_pad
@@ -146,19 +145,6 @@
             acor[1, 1, v, at, :] = spread(up_block, 0, last - 1)
             acor[1, 2, v, at, :] = spread(up_block, 1, last)
             acor[1, 3, v, at, :] = spread(up_block, 1, last - 1)
-            rolled = pltpu.roll(lo_block, 4 * v, 1) if v else lo_block
-            unit = ((lane == 4 * v + 2) & (row == last)) | ((lane == 4 * v + 3) & (row == last - 1))
-            cols = jnp.where((lane == 4 * v) | (lane == 4 * v + 1), rolled, jnp.where(unit, 1.0, 0.0))
-            packed = packed + product(jnp.concatenate([h, o], axis=1), cols)
-        for v in range(nv):
-            for j in range(2):
-                for k in range(2):
-                    cor[j, k, v, at, :] = spread(packed, j, 4 * v + k)
-            scaled = packed * mix[v]
-            h, o = split(scaled)
-            hf = h.astype(F32)
-            stacked = hf + pltpu.roll(o.astype(F32), 32, 1) + pltpu.roll(hf, 64, 1)
-            lhs[p, v * points:(v + 1) * points, :] = stacked.astype(BF16)
         return carry
 
     lax.fori_loop(0, planes, prepare, 0)
@@ -195,7 +181,7 @@
     rhs[slots:2 * slots, nv * width:(nv + 1) * width] = jnp.zeros((slots, width), BF16)
     slot_lane = lax.broadcasted_iota(jnp.int32, (1, cap), 1)
     targets = jnp.concatenate(
-        [jnp.where(slot_lane < counts[s, 0, 0], rrows[0, 0, s:s + 1, :], planes * points) for s in range(np_)], axis=1)
+        [jnp.where(slot_lane < counts[0, 0, s], rrows[0, 0, s:s + 1, :], planes * points) for s in range(np_)], axis=1)
     target_all = jnp.broadcast_to(targets, (points, slots))
     row_slot = lax.broadcasted_iota(jnp.int32, (points, slots), 0)
     wave_in.wait()
@@ -294,6 +280,32 @@
         for j in range(4):
             cfix[j, v] = -wedge[j] * acc[j]
 
+    def pack(p, carry):
+        at = pl.ds(p, 1)
+        packed = jnp.zeros((points, width), F32)
+        for v in range(nv):
+            lo_block = lbuf[v, p]
+            rolled = pltpu.roll(lo_block, 4 * v, 1) if v else lo_block
+            unit = ((lane == 4 * v + 2) & (row == last)) | ((lane == 4 * v + 3) & (row == last - 1))
+            cols = jnp.where((lane == 4 * v) | (lane == 4 * v + 1), rolled, jnp.where(unit, 1.0, 0.0))
+            packed = packed + product(usp[v, p], cols)
+        for v in range(nv):
+            for j in range(2):
+                for k in range(2):
+                    cor[j, k, v, at, :] = spread(packed, j, 4 * v + k)
+        packs[p] = packed
+        return carry
+
+    def scale(p, carry):
+        packed = packs[p]
+        for v in range(nv):
+            scaled = packed * mix[v]
+            h, o = split(scaled)
+            hf = h.astype(F32)
+            stacked = hf + pltpu.roll(o.astype(F32), 32, 1) + pltpu.roll(hf, 64, 1)
+            lhs[p, v * points:(v + 1) * points, :] = stacked.astype(BF16)
+        return carry
+
     def lower_pass(p, carry):
         chunk = p // SUB
         at = pl.ds(p % SUB, 1)
@@ -392,15 +404,36 @@
                 bmine[1, c, j, v] = ubrow[j, v, sl] - cor[j, 0, v, sl] * f - cor[j, 1, v, sl] * s
         b_copy(1, c).start()
 
+    def work(body, c):
+        lax.fori_loop(c * SUB, (c + 1) * SUB, body, 0)
+
+    slots_of = [(pack, c) for c in range(chunks)] + [(upper_pass, c) for c in range(chunks)]
+    for turn in range(len(slots_of) + chunks):
+        for c in range(chunks):
+            spot = turn - c
+            if 0 <= spot < len(slots_of):
+                @pl.when(z == spot if spot < len(slots_of) - 1 else z >= spot)
+                def _():
+                    relay(0, c)
+                if spot == len(slots_of) - 1:
+                    back_offset(c)
+        if turn < len(slots_of):
+            work(*slots_of[turn])
+
+    @pl.when(z == nz - 1)
+    def _():
+        for c in range(chunks):
+            relay(1, c)
+
+    lax.fori_loop(0, planes, scale, 0)
+
+    @pl.when(z < nz - 1)
+    def _():
+        for c in range(chunks):
+            relay(1, c)
+
+    nk = 4 * nv
     for c in range(chunks):
-        lax.fori_loop(c * SUB, (c + 1) * SUB, upper_pass, 0)
-        relay(0, c)
-        back_offset(c)
-
-    nk = 4 * nv
-    out_copies = []
-    for c in range(chunks):
-        relay(1, c)
         sl = slice(c * SUB, (c + 1) * SUB)
         for v in range(nv):
             x1, x2 = fin[1, c, 0, v], fin[1, c, 1, v]
@@ -420,9 +453,6 @@
             return carry
 
         lax.fori_loop(0, SUB, finish, 0)
-        copy = pltpu.make_async_copy(obuf.at[:, pl.ds(c * SUB, SUB)], out.at[:, pl.ds(c * SUB, SUB)], osem.at[c])
-        copy.start()
-        out_copies.append(copy)
 
     for d in peers:
         donor_copy(d).wait_send()
@@ -444,8 +474,6 @@
             @pl.when(has_after(side))
             def _():
                 chain_copy(side, c).wait_send()
-    for copy in out_copies:
-        copy.wait()
 
 
 def local(np_, nl_, flow_state, wave_speed, left_eig, right_eig, lower_inverse, upper_inverse, lower_link, upper_link,
@@ -456,14 +484,14 @@
     slots = np_ * cap
     vmem = pl.BlockSpec(memory_space=pltpu.VMEM)
     smem = pl.BlockSpec(memory_space=pltpu.SMEM)
-    hbm = pl.BlockSpec(memory_space=pl.ANY)
+    hbm = pl.BlockSpec(memory_space=pltpu.HBM)
     dma = pltpu.SemaphoreType.DMA
     state = (2, chunks, 2, nv, SUB, width)
     return pl.pallas_call(
         functools.partial(kernel, np_, nl_),
-        out_shape=jax.ShapeDtypeStruct(flow_state.shape, F32),
+        out_shape=pltpu.VMEM(flow_state.shape, F32),
         in_specs=[hbm, hbm, hbm, hbm, smem, smem, vmem, vmem, smem, smem, smem, smem, vmem],
-        out_specs=hbm,
+        out_specs=vmem,
         scratch_shapes=[
             pltpu.VMEM((nv, planes, points + 2 * PAD, width), F32),
             pltpu.VMEM((planes, points, width), F32),
@@ -472,7 +500,7 @@
             pltpu.VMEM((nv, planes, points, 2 * points), BF16),
             pltpu.VMEM((nv, planes, points, 2 * points), BF16),
             pltpu.VMEM((nv, planes, points, width), F32),
-            pltpu.VMEM((nv, planes, points, width), F32),
+            pltpu.VMEM((planes, points, width), F32),
             pltpu.VMEM((planes, nv * points, width), BF16),
             pltpu.VMEM((np_, nv, cap, width), F32),
             pltpu.VMEM((np_, nv, cap, width), F32),
@@ -491,14 +519,14 @@
             pltpu.VMEM((2, 2, nv, planes, width), F32),
             pltpu.VMEM((2, 4, nv, planes, width), F32),
             pltpu.VMEM((chunks, 4 * nv, SUB, width), F32),
-            dma((4,)), dma((chunks,)), dma((np_,)), dma((np_,)), dma((1,)), dma((2,)), dma((2,)), dma((2,)), dma((2,)),
+            dma((4,)), dma((np_,)), dma((np_,)), dma((1,)), dma((2,)), dma((2,)), dma((2,)), dma((2,)),
             dma((2, chunks)), dma((2, chunks)), dma((2, chunks)), dma((2, chunks)),
         ],
         compiler_params=pltpu.CompilerParams(
-            collective_id=0, has_side_effects=True, vmem_limit_bytes=60 * 1024 * 1024),
+            collective_id=0, has_side_effects=True, vmem_limit_bytes=54 * 1024 * 1024),
     )(flow_state, wave_speed, lower_inverse, upper_inverse, left_eig, right_eig,
       lower_link.reshape(lower_link.shape[:3] + (width,)), upper_link.reshape(upper_link.shape[:3] + (width,)),
-      donor_rows, stencil_offsets, donor_weights, block_counts, receptor_rows)
+      donor_rows, stencil_offsets, donor_weights, jnp.transpose(block_counts, (1, 2, 0)), receptor_rows)
 
 
 def solution(mesh):

time: 68.4 us -> 57.6 us (0.84)
  Pallas kernels: 61.5 us -> 55.1 us
  local copies, waits for them, and re-layouts: 6.8 us -> 2.36 us
    pallas_call x1, Pallas kernels: 61.5 us -> 55.1 us  [local(): pl.pallas_call(functools.partial(kernel, np_, nl_), out_shape=pltpu.VMEM(...]
    unnamed x2 -> x1, local copies, waits for them, and re-layouts: 6.8 us -> 2.36 us
where the time goes in v1:
time: 57.6 us; the launch traced here: 57.5 us
  Pallas kernels  55.1 us (96%)
  local copies, waits for them, and re-layouts  2.36 us (4%)
    pallas_call x1, Pallas kernels, local(): pl.pallas_call(functools.partial(kernel, np_, nl_), out_shape=pltpu.VMEM(...  55.1 us
    unnamed x1, local copies, waits for them, and re-layouts  2.36 us

profile of v1, /device:TPU:0, one launch (start us, length us, event | category | flops | bytes accessed | tf_op | source)
XLA Modules:
  0.0 57.5 jit_solution(4577314417568275138)
XLA Ops:
  0.0 55.1 %shard_map.127 = f32[5,16,128,128]{3,2,1,0:T(8,128)S(1)} custom-call(f32[5,16,128,128]{3,2,1,0:T(8,128)} %flow.1, f32[16,128,128]{2,1,0:T(8,128)} %wave.1, f32[5,16,128,128]{3,2,1,0:T(8,128)} %lower.1, f32[5,16,128,128]{3,2,1,0:T(8,128)} %upper.1, f32[5,5]{1,0:T(8,128)} %left_eig.1, f32[5,5]{1,0:T(8,128)} %right_eig.1, f32[3,5,16,128]{3,2,1,0:T(8,128)} %bitcast.3, ...), custom_call_target="tpu_custom_call" | custom-call | tf_op jit(solution)/shard_map/pallas_call | solution.py:490
  55.1 2.4 %copy.15 = f32[5,16,128,128]{3,2,1,0:T(8,128)} copy(f32[5,16,128,128]{3,2,1,0:T(8,128)S(1)} %shard_map.127) | data formatting | bytes 10485760
